TPU v7x, 32 devices: a whole 2x2x4 slice. The times are simulated.
32 devices in a mesh: groups: 2 (over y), expert: 4 (over z), tensor: 4 (over x, core).
Axes of the slice: x: 2, y: 2, z: 4, core: 2. Of those that a mesh axis runs over, the one named last changes fastest.
Arguments:
- tokens: bfloat16 [256, 4096], P(('groups', 'expert')), parts along dimension 0, may hold values from -6 to 6
- route_ids: int32 [256, 2], P(('groups', 'expert')), parts along dimension 0, may hold values from 0 to 3, all different within a row; in each aligned block of 32 rows (0 to 31, 32 to 63, ...) at most 24 rows name the same one
- route_gates: float32 [256, 2], P(('groups', 'expert')), parts along dimension 0, may hold values from 0.1 to 1
- gate_weight: bfloat16 [4096, 32768], P(None, ('expert', 'tensor')), may hold values from -0.09375 to 0.09375
- up_weight: bfloat16 [4096, 32768], P(None, ('expert', 'tensor')), may hold values from -0.09375 to 0.09375
- down_weight: bfloat16 [32768, 4096], P('expert', 'tensor'), may hold values from -0.0625 to 0.0625
Outputs:
- mixed: bfloat16 [256, 4096], P(('groups', 'expert'), 'tensor'), parts along dimension 0
There are 2 independent parts, one for each index of `groups`. A program takes and returns all parts, laid end to end along the dimension named above; an argument that names none is the same for every part. Nothing has to cross between parts.
Inputs may be any that keep to these rules, and one draw needn't show every extreme that they name: `route_ids`: each row names 2 different experts. In the rows of one device no expert is named more than 24 times, and in some device's rows one expert is named exactly 24 times.
All inputs are finite; a program needn't handle non-finite values.
Results may differ from a plain program's by a relative error of at most 0.005.
Values may be sent and summed in bfloat16 or wider, within the bound.
A program may use at most 128 MiB of HBM per device.

v0:
```python
import functools

import jax
import jax.numpy as jnp
from jax import lax
from jax.experimental import pallas as pl
from jax.experimental.pallas import tpu as pltpu
from jax.sharding import PartitionSpec as P

EXPERTS = 4
CAP = 24
EPSILON = 1e-05
LAG = 4
MESH = pl.DeviceIdType.MESH
F32 = jnp.float32
BF16 = jnp.bfloat16


def kernel(
    n_e, n_t, chunks,
    tok_hbm, ids_hbm, gates_hbm, wg_hbm, wu_hbm, wd_hbm, out_ref,
    tok, ids, gates, normed, pick_t, combine, pack, recv, xs, wg, wu, wd, hid, acc, back, ret,
    small_sem, wg_sem, wu_sem, wd_sem,
    p1_send, p1_recv, p2x_send, p2c_send, p3_send, p2_recv,
    hx_send, hc_send, h3_send, h_recv, r_send, r_recv,
):
    e = lax.axis_index("expert")
    t = lax.axis_index("tensor")
    n_x = n_t // 2
    xi, core = t // 2, t % 2
    mate = xi * 2 + 1 - core
    blocks = n_e // EXPERTS
    rows, width = tok.shape
    sw = width // n_t
    served = n_e * CAP
    cw = hid.shape[3]
    hidden = wd.shape[0]

    def xpeer(d):
        return lax.rem(xi + d, n_x) * 2 + core

    def xmate(d):
        return lax.rem(xi + d, n_x) * 2 + 1 - core

    hops = sorted(range(1, n_e), key=lambda d: (abs(2 * d - n_e), d))
    far = list(range(1, n_x))

    smalls = [
        pltpu.make_async_copy(tok_hbm, tok, small_sem.at[0]),
        pltpu.make_async_copy(ids_hbm, ids, small_sem.at[1]),
        pltpu.make_async_copy(gates_hbm, gates, small_sem.at[2]),
    ]
    for c in smalls:
        c.start()

    barrier = pltpu.get_barrier_semaphore()
    for d in hops:
        pl.semaphore_signal(barrier, inc=1, device_id={"expert": lax.rem(e + d, n_e)}, device_id_type=MESH)
    for d in far:
        pl.semaphore_signal(barrier, inc=1, device_id={"tensor": xpeer(d)}, device_id_type=MESH)
    pl.semaphore_signal(barrier, inc=1, device_id={"tensor": mate}, device_id_type=MESH)

    def weight_copies(k):
        cols = pl.ds(k * cw, cw)
        return (
            pltpu.make_async_copy(wg_hbm.at[:, cols], wg.at[k], wg_sem.at[k]),
            pltpu.make_async_copy(wu_hbm.at[:, cols], wu.at[k], wu_sem.at[k]),
        )

    for k in range(chunks):
        for c in weight_copies(k):
            c.start()
    part = hidden // n_t
    downs = [
        pltpu.make_async_copy(wd_hbm.at[pl.ds(s * part, part)], wd.at[pl.ds(s * part, part)], wd_sem.at[s])
        for s in range(n_t)
    ]
    for c in downs:
        c.start()

    for c in smalls:
        c.wait()
    floats = tok[...].astype(F32)
    scale = lax.rsqrt(jnp.mean(floats * floats, axis=-1, keepdims=True) + EPSILON)
    normed[...] = (floats * scale).astype(BF16)
    slots = EXPERTS * CAP
    row = lax.broadcasted_iota(jnp.int32, (slots, rows), 0)
    of = jnp.zeros((slots, rows), jnp.int32)
    for x in range(1, EXPERTS):
        of = of + (row >= x * CAP).astype(jnp.int32)
    at = row - of * CAP
    named = [(ids[k : k + 1, :] == of).astype(F32) for k in range(ids.shape[0])]
    mask = functools.reduce(jnp.add, named)
    above = (
        lax.broadcasted_iota(jnp.int32, (rows, rows), 0) < lax.broadcasted_iota(jnp.int32, (rows, rows), 1)
    ).astype(F32)
    position = jnp.dot(mask.astype(BF16), above.astype(BF16), preferred_element_type=F32)
    hit = (position == at.astype(F32)).astype(F32)
    pick_t[...] = mask * hit
    mine = pl.ds(pl.multiple_of(t * sw, 128), sw)
    packed = jnp.dot(pick_t[...].astype(BF16), normed[:, mine], preferred_element_type=F32)
    for x in range(EXPERTS):
        pack[x] = packed[x * CAP : (x + 1) * CAP].astype(BF16)

    pl.semaphore_wait(barrier, len(hops) + len(far) + 1)

    def p1(src_e, dst_e, source):
        return pltpu.make_async_remote_copy(
            src_ref=pack.at[dst_e // blocks], dst_ref=recv.at[t, source],
            send_sem=p1_send.at[dst_e], recv_sem=p1_recv.at[source],
            device_id={"expert": dst_e}, device_id_type=MESH,
        )

    for d in hops:
        p1(e, lax.rem(e + d, n_e), e).start()

    weight = functools.reduce(jnp.add, [named[k] * gates[k : k + 1, :] for k in range(ids.shape[0])])
    combine[...] = (weight * hit).T
    own = pick_t[pl.ds(pl.multiple_of((e // blocks) * CAP, 8), CAP), :].astype(BF16)
    for s in range(n_t):
        recv[s, e] = jnp.dot(own, normed[:, s * sw : (s + 1) * sw], preferred_element_type=F32).astype(BF16)

    def move(ref, sends, recvs, send_at, slot, target):
        return pltpu.make_async_remote_copy(
            src_ref=ref.at[slot], dst_ref=ref.at[slot],
            send_sem=sends.at[send_at], recv_sem=recvs.at[slot],
            device_id={"tensor": target}, device_id_type=MESH,
        )

    sources = [lax.rem(e + n_e - d, n_e) for d in hops]
    for j in sources:
        p1(j, j, j).wait_recv()
        for d in far:
            move(recv, p2x_send, p2_recv, (d, j), (t, j), xpeer(d)).start()
        move(recv, p2c_send, p2_recv, j, (t, j), mate).start()
    def fill(s):
        flat = recv[s].astype(F32).reshape(served, sw).astype(BF16)
        xs[:, pl.ds(pl.multiple_of(s * sw, 128), sw)] = flat

    fill(t)
    for j in sources:
        for d in far:
            move(recv, p3_send, p2_recv, (d, j), (xpeer(d), j), mate).wait_recv()
            move(recv, p3_send, p2_recv, (d, j), (xpeer(d), j), mate).start()
    for d in far:
        fill(xpeer(d))
    for j in sources:
        move(recv, p2c_send, p2_recv, j, (mate, j), mate).wait_recv()
    fill(mate)
    for d in far:
        for j in sources:
            move(recv, p3_send, p2_recv, (d, j), (xmate(d), j), mate).wait_recv()
        fill(xmate(d))

    def relay(k):
        for d in far:
            c = move(hid, h3_send, h_recv, (d, k), (xpeer(d), k), mate)
            c.wait_recv()
            c.start()

    def gate_up(k, carry):
        for c in weight_copies(k):
            c.wait()
        g = jnp.dot(xs[...], wg[k], preferred_element_type=F32)
        u = jnp.dot(xs[...], wu[k], preferred_element_type=F32)
        hid[t, k] = (g / (1.0 + jnp.exp(-g)) * u).astype(BF16)
        for d in far:
            move(hid, hx_send, h_recv, (d, k), (t, k), xpeer(d)).start()
        move(hid, hc_send, h_recv, k, (t, k), mate).start()

        @pl.when(k >= LAG)
        def _():
            relay(k - LAG)

        return carry

    lax.fori_loop(0, chunks, gate_up, 0)
    for c in downs:
        c.wait()
    acc[...] = jnp.zeros_like(acc)

    def down(s, first, last, waits):
        def step(k, carry):
            if waits is not None:
                waits(k)
            at_row = pl.ds(pl.multiple_of((s * chunks + k) * cw, 128), cw)
            acc[...] += jnp.dot(hid[s, k], wd[at_row, :], preferred_element_type=F32)
            return carry

        lax.fori_loop(first, last, step, 0)

    def from_mate(slot_of):
        return lambda k: move(hid, hc_send, h_recv, k, (slot_of, k), mate).wait_recv()

    down(t, 0, chunks, None)
    late = list(range(max(0, chunks - LAG), chunks))
    cuts = [chunks * i // len(late) for i in range(len(late) + 1)]
    for i, k in enumerate(late):
        relay(k)
        down(mate, cuts[i], cuts[i + 1], from_mate(mate))
    for d in far:
        down(xpeer(d), 0, chunks, None)
    for d in far:
        down(xmate(d), 0, chunks, from_mate(xmate(d)))

    for j in range(n_e):
        back[j] = acc[j * CAP : (j + 1) * CAP, :].astype(BF16)

    def giving(dst_e, source):
        return pltpu.make_async_remote_copy(
            src_ref=back.at[dst_e], dst_ref=ret.at[source],
            send_sem=r_send.at[dst_e], recv_sem=r_recv.at[source],
            device_id={"expert": dst_e}, device_id_type=MESH,
        )

    for d in hops:
        giving(lax.rem(e + d, n_e), e).start()
    ret[e] = back[e]

    for d in hops:
        p1(e, lax.rem(e + d, n_e), e).wait_send()
    for j in sources:
        for d in far:
            move(recv, p2x_send, p2_recv, (d, j), (t, j), xpeer(d)).wait_send()
            move(recv, p3_send, p2_recv, (d, j), (xpeer(d), j), mate).wait_send()
        move(recv, p2c_send, p2_recv, j, (t, j), mate).wait_send()

    def drain(k, carry):
        for d in far:
            move(hid, hx_send, h_recv, (d, k), (t, k), xpeer(d)).wait_send()
            move(hid, h3_send, h_recv, (d, k), (xpeer(d), k), mate).wait_send()
        move(hid, hc_send, h_recv, k, (t, k), mate).wait_send()
        return carry

    lax.fori_loop(0, chunks, drain, 0)

    for j in sources:
        giving(j, j).wait_recv()
    parts = []
    for x in range(EXPERTS):
        total = ret[x * blocks].astype(F32)
        for b in range(1, blocks):
            total = total + ret[x * blocks + b].astype(F32)
        parts.append(total)
    mixture = jnp.dot(
        combine[...], jnp.concatenate(parts, axis=0),
        precision=lax.Precision.HIGHEST, preferred_element_type=F32,
    )
    out_ref[...] = (tok[:, mine].astype(F32) + mixture).astype(BF16)
    for d in hops:
        giving(lax.rem(e + d, n_e), e).wait_send()


def solution(mesh):
    n_e, n_t = mesh.shape["expert"], mesh.shape["tensor"]

    def local(tokens, route_ids, route_gates, gate_weight, up_weight, down_weight):
        rows, width = tokens.shape
        own_hidden = gate_weight.shape[1]
        hidden, out_w = down_weight.shape
        sw = width // n_t
        cw = min(256, own_hidden)
        chunks = own_hidden // cw
        served = n_e * CAP
        dma = pltpu.SemaphoreType.DMA
        n_x = n_t // 2
        scratch = [
            pltpu.VMEM((rows, width), BF16),
            pltpu.VMEM(route_ids.shape[::-1], jnp.int32),
            pltpu.VMEM(route_gates.shape[::-1], F32),
            pltpu.VMEM((rows, width), BF16),
            pltpu.VMEM((EXPERTS * CAP, rows), F32),
            pltpu.VMEM((rows, EXPERTS * CAP), F32),
            pltpu.VMEM((EXPERTS, CAP, sw), BF16),
            pltpu.VMEM((n_t, n_e, CAP, sw), BF16),
            pltpu.VMEM((served, width), BF16),
            pltpu.VMEM((chunks, width, cw), BF16),
            pltpu.VMEM((chunks, width, cw), BF16),
            pltpu.VMEM((hidden, out_w), BF16),
            pltpu.VMEM((n_t, chunks, served, cw), BF16),
            pltpu.VMEM((served, out_w), F32),
            pltpu.VMEM((n_e, CAP, out_w), BF16),
            pltpu.VMEM((n_e, CAP, out_w), BF16),
            dma((3,)), dma((chunks,)), dma((chunks,)), dma((n_t,)),
            dma((n_e,)), dma((n_e,)), dma((n_x, n_e)), dma((n_e,)), dma((n_x, n_e)), dma((n_t, n_e)),
            dma((n_x, chunks)), dma((chunks,)), dma((n_x, chunks)), dma((n_t, chunks)), dma((n_e,)), dma((n_e,)),
        ]
        return pl.pallas_call(
            functools.partial(kernel, n_e, n_t, chunks),
            out_shape=jax.ShapeDtypeStruct((rows, out_w), BF16),
            in_specs=[pl.BlockSpec(memory_space=pl.ANY)] * 6,
            out_specs=pl.BlockSpec(memory_space=pltpu.VMEM),
            scratch_shapes=scratch,
            compiler_params=pltpu.CompilerParams(
                collective_id=0, has_side_effects=True, vmem_limit_bytes=57_000_000
            ),
        )(tokens, route_ids.T, route_gates.T, gate_weight, up_weight, down_weight)

    in_specs = (
        P(("groups", "expert"), None),
        P(("groups", "expert"), None),
        P(("groups", "expert"), None),
        P(None, ("expert", "tensor")),
        P(None, ("expert", "tensor")),
        P("expert", "tensor"),
    )
    return jax.shard_map(
        local, mesh=mesh, in_specs=in_specs, out_specs=P(("groups", "expert"), "tensor"), check_vma=False
    )
```

profile of v0, /device:TPU:0, one launch (start us, length us, event | category | flops | bytes accessed | tf_op | source)
XLA Modules:
  0.0 39.4 jit_solution(9600235681606827896)
XLA Ops:
  0.0 37.9 %shard_map.64 = bf16[32,1024]{1,0:T(8,128)(2,1)} custom-call(bf16[32,4096]{1,0:T(8,128)(2,1)} %tok_hbm.1, s32[2,32]{1,0:T(2,128)} %bitcast.2, f32[2,32]{1,0:T(2,128)} %bitcast.3, bf16[4096,2048]{1,0:T(8,128)(2,1)} %wg_hbm.1, bf16[4096,2048]{1,0:T(8,128)(2,1)} %wu_hbm.1, bf16[8192,1024]{1,0:T(8,128)(2,1)} %wd_hbm.1), custom_call_target="tpu_custom_call" | custom-call | tf_op jit(solution)/shard_map/pallas_call | solution.py:288
  37.9 1.5 %copy.8 = bf16[32,1024]{1,0:T(8,128)(2,1)} copy(bf16[32,1024]{1,0:T(8,128)(2,1)} %shard_map.64) | data formatting | bytes 131072
where the time goes:
time: 39.6 us; the launch traced here: 39.4 us
  Pallas kernels  37.9 us (96%)
  local copies, waits for them, and re-layouts  1.47 us (4%)
    pallas_call x1, Pallas kernels, local(): pl.pallas_call(functools.partial(kernel, n_e, n_t, chunks), out_shape=jax...  37.9 us
    unnamed x1, local copies, waits for them, and re-layouts  1.47 us

commit v1 on v0

--- a/solution.py
+++ b/solution.py
@@ -158,7 +158,7 @@
             c.wait_recv()
             c.start()
 
-    def gate_up(k, carry):
+    def gate_up(k):
         for c in weight_copies(k):
             c.wait()
         g = jnp.dot(xs[...], wg[k], preferred_element_type=F32)
@@ -168,40 +168,41 @@
             move(hid, hx_send, h_recv, (d, k), (t, k), xpeer(d)).start()
         move(hid, hc_send, h_recv, k, (t, k), mate).start()
 
-        @pl.when(k >= LAG)
-        def _():
+    for k in range(chunks):
+        gate_up(k)
+        if k >= LAG:
             relay(k - LAG)
-
-        return carry
-
-    lax.fori_loop(0, chunks, gate_up, 0)
     for c in downs:
         c.wait()
-    acc[...] = jnp.zeros_like(acc)
-
-    def down(s, first, last, waits):
-        def step(k, carry):
-            if waits is not None:
-                waits(k)
+
+    def down(s, ks):
+        total = None
+        for k in ks:
             at_row = pl.ds(pl.multiple_of((s * chunks + k) * cw, 128), cw)
-            acc[...] += jnp.dot(hid[s, k], wd[at_row, :], preferred_element_type=F32)
-            return carry
-
-        lax.fori_loop(first, last, step, 0)
-
-    def from_mate(slot_of):
-        return lambda k: move(hid, hc_send, h_recv, k, (slot_of, k), mate).wait_recv()
-
-    down(t, 0, chunks, None)
-    late = list(range(max(0, chunks - LAG), chunks))
-    cuts = [chunks * i // len(late) for i in range(len(late) + 1)]
+            part = jnp.dot(hid[s, k], wd[at_row, :], preferred_element_type=F32)
+            total = part if total is None else total + part
+        return total
+
+    def from_mate(slot_of, ks):
+        for k in ks:
+            move(hid, hc_send, h_recv, k, (slot_of, k), mate).wait_recv()
+
+    every = list(range(chunks))
+    acc[...] = down(t, every)
+    late = every[max(0, chunks - LAG) :]
     for i, k in enumerate(late):
         relay(k)
-        down(mate, cuts[i], cuts[i + 1], from_mate(mate))
-    for d in far:
-        down(xpeer(d), 0, chunks, None)
-    for d in far:
-        down(xmate(d), 0, chunks, from_mate(xmate(d)))
+        if i == 0:
+            from_mate(mate, every)
+            acc[...] += down(mate, every)
+    half = max(1, chunks // 2)
+    for d in far:
+        acc[...] += down(xpeer(d), every)
+    for d in far:
+        for ks in (every[:half], every[half:]):
+            if ks:
+                from_mate(xmate(d), ks)
+                acc[...] += down(xmate(d), ks)
 
     for j in range(n_e):
         back[j] = acc[j * CAP : (j + 1) * CAP, :].astype(BF16)

time: 39.6 us -> 37 us (0.934)
  Pallas kernels: 37.9 us -> 35.3 us
    pallas_call x1, Pallas kernels: 37.9 us -> 35.3 us  [local(): pl.pallas_call(functools.partial(kernel, n_e, n_t, chunks), out_shape=jax...]
where the time goes in v1:
time: 37 us; the launch traced here: 36.8 us
  Pallas kernels  35.3 us (95%)
  local copies, waits for them, and re-layouts  1.47 us (4%)
    pallas_call x1, Pallas kernels, local(): pl.pallas_call(functools.partial(kernel, n_e, n_t, chunks), out_shape=jax...  35.3 us
    unnamed x1, local copies, waits for them, and re-layouts  1.47 us

profile of v1, /device:TPU:0, one launch (start us, length us, event | category | flops | bytes accessed | tf_op | source)
XLA Modules:
  0.0 36.8 jit_solution(285707714287666851)
XLA Ops:
  0.0 35.3 %shard_map.64 = bf16[32,1024]{1,0:T(8,128)(2,1)} custom-call(bf16[32,4096]{1,0:T(8,128)(2,1)} %tok_hbm.1, s32[2,32]{1,0:T(2,128)} %bitcast.2, f32[2,32]{1,0:T(2,128)} %bitcast.3, bf16[4096,2048]{1,0:T(8,128)(2,1)} %wg_hbm.1, bf16[4096,2048]{1,0:T(8,128)(2,1)} %wu_hbm.1, bf16[8192,1024]{1,0:T(8,128)(2,1)} %wd_hbm.1), custom_call_target="tpu_custom_call" | custom-call | tf_op jit(solution)/shard_map/pallas_call | solution.py:289
  35.3 1.5 %copy.8 = bf16[32,1024]{1,0:T(8,128)(2,1)} copy(bf16[32,1024]{1,0:T(8,128)(2,1)} %shard_map.64) | data formatting | bytes 131072
